TPU v7x, 32 devices: a whole 2x2x4 slice. The times are simulated.
32 devices in a mesh: src: 16 (over z, y, core), sub: 2 (over x).
Axes of the slice: x: 2, y: 2, z: 4, core: 2. Of those that a mesh axis runs over, the one named last changes fastest.
Arguments:
- child_rhs: float32 [2, 1024, 4096], P('sub', None, 'src'), may hold values from -6 to 6
- root_rhs: float32 [2048, 4096], P('sub', 'src'), may hold values from -6 to 6
- child_inverse: bfloat16 [2, 1024, 1024], P('sub', 'src'), as said below
- coupling_block: bfloat16 [2, 1024, 1024], P('sub', 'src'), may hold values from -0.1875 to 0.1875
- root_inverse: bfloat16 [2048, 2048], P('sub', 'src'), as said below
- child_orders: int32 [2], P('sub'), may hold values from 716 to 1024, as said below
- coupling_rows: int32 [2, 1024], P('sub'), may hold values from 0 to 2047, as said below
Outputs:
- child_solution: float32 [2, 1024, 4096], P('sub', None, 'src')
- root_solution: float32 [2048, 4096], P('sub', 'src')
Inputs may be any that keep to these rules, and one draw needn't show every extreme that they name: Each child_inverse[j] is lower triangular: zero above the diagonal, diagonal entries between 0.8 and 1.25. `root_inverse`: lower triangular: zero above the diagonal, diagonal entries between 0.8 and 1.25. `coupling_rows`: each row holds 1024 distinct root rows in increasing order. `child_orders`: some child has order 1024.
All inputs are finite; a program needn't handle non-finite values.
Results may differ from a plain program's by a relative error of at most 0.0093.
Values may be sent and summed in bfloat16 or wider, within the bound.
A program may use at most 64 MiB of HBM per device.

v0:
```python
import jax
import jax.numpy as jnp
from jax import lax
from jax.sharding import PartitionSpec as P


def contract_rows(left, right):
    return lax.dot_general(
        left, right, (((0,), (0,)), ((), ())), preferred_element_type=jnp.float32
    )


def on_device(
    child_rhs, root_rhs, child_inverse, coupling_block, root_inverse, child_orders, coupling_rows
):
    inverse = child_inverse[0]
    coupling = coupling_block[0]
    coupling_index = coupling_rows[0]
    columns = child_rhs.shape[2]
    child_order = inverse.shape[1]
    block_rows = root_rhs.shape[0]
    root_order = root_inverse.shape[1] * lax.axis_size("src")
    alive = (lax.iota(jnp.int32, child_order) < child_orders[0])[:, None]
    child_source = jnp.where(alive, child_rhs[0], 0.0).astype(jnp.bfloat16)
    forward = jnp.dot(
        lax.all_gather(inverse, "src", axis=0, tiled=True),
        child_source,
        preferred_element_type=jnp.float32,
    )
    child_solved = jnp.where(alive, forward, 0.0)
    solved_round = child_solved.astype(jnp.bfloat16)
    update = jnp.dot(
        lax.all_gather(coupling, "src", axis=0, tiled=True),
        solved_round,
        preferred_element_type=jnp.float32,
    )
    placed = jnp.zeros((root_order, columns), jnp.float32).at[coupling_index].add(update)
    first_row = lax.axis_index("sub") * block_rows
    own_rows = lax.dynamic_slice_in_dim(placed, first_row, block_rows, 0)
    summand = lax.dynamic_update_slice_in_dim(-placed, root_rhs - own_rows, first_row, 0)
    root_source = lax.psum(summand, "sub").astype(jnp.bfloat16)
    root_forward = jnp.dot(
        lax.all_gather(root_inverse, "src", axis=1, tiled=True),
        root_source,
        preferred_element_type=jnp.float32,
    )
    root_round = root_forward.astype(jnp.bfloat16)
    partial_root = contract_rows(
        lax.all_gather(root_inverse, "src", axis=1, tiled=True), root_round
    )
    root_out = lax.psum_scatter(partial_root, "sub", scatter_dimension=0, tiled=True)
    rounded_all = lax.all_gather(root_out.astype(jnp.bfloat16), "sub", axis=0, tiled=True)
    picked = rounded_all[coupling_index]
    pulled = contract_rows(lax.all_gather(coupling, "src", axis=0, tiled=True), picked)
    residue = jnp.where(alive, child_solved - pulled, 0.0).astype(jnp.bfloat16)
    backward = contract_rows(lax.all_gather(inverse, "src", axis=0, tiled=True), residue)
    child_out = jnp.where(alive, backward, 0.0)[None]
    return (child_out, root_out)


def solution(mesh):
    return jax.shard_map(
        on_device,
        mesh=mesh,
        in_specs=(
            P("sub", None, "src"),
            P("sub", "src"),
            P("sub", "src", None),
            P("sub", "src", None),
            P("sub", "src"),
            P("sub"),
            P("sub", None),
        ),
        out_specs=(P("sub", None, "src"), P("sub", "src")),
        check_vma=False,
    )
```

profile of v0, /device:TPU:0, one launch (start us, length us, event | category | flops | bytes accessed | tf_op | source)
XLA Modules:
  0.0 242.1 jit_solution(16274058468661391291)
XLA Ops:
  7.2 0.0 all-gather.11.cloned.1.call-start
  7.2 0.7 all-gather.11.cloned.1.call-update
  7.9 0.0 all-gather.13.cloned.1.call-start
  7.9 0.7 all-gather.13.cloned.1.call-update
  8.6 0.0 all-gather.7.cloned.1.call-start
  8.7 0.7 all-gather.7.cloned.1.call-update
  9.4 0.0 reduce-scatter.2.cloned.1.call-start
  10.1 0.7 compare_select_fusion
  10.8 43.6 %all-gather.11.cloned.1.call-done = bf16[1,1024,1024]{2,1,0:T(8,128)(2,1)} async-done(((bf16[1,64,1024]{2,1,0:T(8,128)(2,1)}), bf16[1,1024,1024]{2,1,0:T(8,128)(2,1)}) %all-gather.11.cloned.1.call-update) | async-done | bytes 2097168 | tf_op jit(solution)/shard_map/all_gather | solution.py:56
  54.3 2.9 %fusion.11 = f32[256,1024]{1,0:T(8,128)S(1)} fusion(bf16[1,1024,1024]{2,1,0:T(8,128)(2,1)} %all-gather.11.cloned.1.call-done, f32[1,1024,256]{2,1,0:T(8,128)} %param.7, pred[1024]{0:T(1024)(128)(4,1)S(1)} %iota_compare_fusion), kind=kOutput, calls=%fused_computation.12 | convolution fusion | flops 537395200 | bytes 4195328 | tf_op jit(solution)/shard_map/dot_general | solution.py:25
  57.3 39.5 %all-gather.13.cloned.1.call-done = bf16[1,1024,1024]{2,1,0:T(8,128)(2,1)} async-done(((bf16[1,64,1024]{2,1,0:T(8,128)(2,1)}), bf16[1,1024,1024]{2,1,0:T(8,128)(2,1)}) %all-gather.13.cloned.1.call-update) | async-done | bytes 2097168 | tf_op jit(solution)/shard_map/all_gather | solution.py:54
  96.7 2.3 fusion.8
  99.1 1.3 copy.13
  100.4 7.0 %scatter_custom_fusion = f32[2048,256]{1,0:T(8,128)S(1)} fusion(s32[1024]{0:T(1024)S(1)} %bitcast.48, f32[1024,256]{1,0:T(8,128)} %copy.13, f32[]{:T(128)} %constant.5.clone.1), kind=kCustom, calls=%fused_computation.23 | custom fusion | flops 262144 | bytes 2097664 | tf_op jit(solution)/shard_map/scatter-add | solution.py:37
  107.4 0.0 copy-start.1
  107.4 1.5 neg.3
  108.9 0.1 copy-done.1
  109.0 1.2 subtract_dynamic-update-slice_fusion
  110.2 54.1 %all-reduce.1 = bf16[2048,256]{1,0:T(8,128)(2,1)S(1)} all-reduce(f32[2048,256]{1,0:T(8,128)} %subtract_dynamic-update-slice_fusion), channel_id=1, replica_groups=mesh['src'=16,'sub'=2] {'sub'}, use_global_device_ids=true, to_apply=%region_1.2 | all-reduce | flops 524288 | bytes 3145728 | tf_op jit(solution)/shard_map/psum | solution.py:41
  164.3 0.0 all-gather.7.cloned.1.call-done
  164.3 7.2 %convolution_bitcast_fusion = f32[2048,256]{0,1:T(8,128)} fusion(bf16[1024,2048]{1,0:T(8,128)(2,1)} %all-gather.7.cloned.1.call-done, bf16[2048,256]{1,0:T(8,128)(2,1)S(1)} %all-reduce.1), kind=kOutput, calls=%fused_computation.2 | convolution fusion | flops 2147745792 | bytes 7340032 | tf_op jit(solution)/shard_map/dot_general | solution.py:8
  171.6 0.0 reduce-scatter.2.cloned.1.call-update
  171.6 0.0 all-gather.9.cloned.1.call-start
  171.6 30.1 %reduce-scatter.2.cloned.1.call-done = f32[1024,256]{0,1:T(8,128)} async-done(((f32[2048,256]{0,1:T(8,128)}), f32[1024,256]{0,1:T(8,128)}) %reduce-scatter.2.cloned.1.call-update) | async-done | bytes 1048592 | tf_op jit(solution)/shard_map/reduce_scatter | solution.py:51
  201.7 0.0 copy-start
  201.7 2.2 convert_element_type.25
  203.9 0.0 all-gather.9.cloned.1.call-update
  203.9 0.0 copy-done
  203.9 1.3 copy.16
  205.2 20.1 %all-gather.9.cloned.1.call-done = bf16[2048,256]{0,1:T(8,128)(2,1)} async-done(((bf16[1024,256]{0,1:T(8,128)(2,1)}), bf16[2048,256]{0,1:T(8,128)(2,1)}) %all-gather.9.cloned.1.call-update) | async-done | bytes 1048592 | tf_op jit(solution)/shard_map/all_gather | solution.py:52
  225.3 1.5 copy.14
  226.8 3.9 %gather_fusion = bf16[1024,256]{1,0:T(8,128)(2,1)S(1)} fusion(bf16[2048,256]{1,0:T(8,128)(2,1)S(1)} %copy.14, s32[1024]{0:T(1024)S(1)} %broadcast_clamp_fusion), kind=kCustom, calls=%fused_computation | custom fusion | bytes 1052672 | tf_op jit(solution)/shard_map/gather | solution.py:53
  230.8 3.5 %fusion.17 = f32[1,1024,256]{1,2,0:T(8,128)S(1)} fusion(bf16[1,1024,1024]{2,1,0:T(8,128)(2,1)} %all-gather.11.cloned.1.call-done, f32[256,1024]{1,0:T(8,128)S(1)} %fusion.11, bf16[1024,256]{1,0:T(8,128)(2,1)S(1)} %gather_fusion, bf16[1,1024,1024]{2,1,0:T(8,128)(2,1)} %all-gather.13.cloned.1.call-done, pred[1024]{0:T(1024)(128)(4,1)S(1)} %iota_compare_fusion), kind=kOutput, calls=%fused_computation.14 | convolution fusion | flops 1074790400 | bytes 6816768 | tf_op jit(solution)/shard_map/dot_general | solution.py:8
  234.3 1.3 copy.15
  (2 shorter events, 0.0 us)
Async XLA Ops:
  7.2 47.2 %all-gather.11.cloned.1.call-start = ((), (), s32[]{:S(2)}) async-start(), calls=%async_computation.4 | async-start | bytes 2228224 | tf_op jit(solution)/shard_map/all_gather | solution.py:56
  7.9 88.8 %all-gather.13.cloned.1.call-start = ((), (), s32[]{:S(2)}) async-start(), calls=%async_computation.5 | async-start | bytes 2228224 | tf_op jit(solution)/shard_map/all_gather | solution.py:54
  8.6 155.7 %all-gather.7.cloned.1.call-start = ((), (), s32[]{:S(2)}) async-start(), calls=%async_computation.1 | async-start | bytes 4456448 | tf_op jit(solution)/shard_map/all_gather | solution.py:49
  9.4 192.3 %reduce-scatter.2.cloned.1.call-start = ((), (), s32[]{:S(2)}) async-start(), calls=%async_computation.2 | async-start | bytes 3145728 | tf_op jit(solution)/shard_map/reduce_scatter | solution.py:51
  107.4 1.6 copy-start.1
  171.6 53.8 %all-gather.9.cloned.1.call-start = ((), (), s32[]{:S(2)}) async-start(), calls=%async_computation.3 | async-start | bytes 1572864 | tf_op jit(solution)/shard_map/all_gather | solution.py:52
  201.7 2.2 copy-start
Sparse Core Ops, SparseCore 0:
  10.1 44.1 all-gather.10
  56.5 40.1 all-gather.12
  98.9 51.1 all-gather.6
  171.7 29.9 reduce-scatter.1
  204.0 21.2 all-gather.8
where the time goes:
time: 242 us
  waiting for transfers between devices  135 us (56%)
  blocking collectives  54.1 us (22%)
  matrix products  16 us (7%)
  between operations  14.5 us (6%)
  other arithmetic  12.6 us (5%)
  local copies, waits for them, and re-layouts  9.44 us (4%)
    psum x1, blocking collectives, on_device(): root_source = lax.psum(summand, 'sub').astype(jnp.bfloat16)  54.1 us
    all_gather x1, waiting for transfers between devices, on_device(): lax.all_gather(inverse, 'src', axis=0, tiled=True)  43.6 us
    all_gather x1, waiting for transfers between devices, on_device(): lax.all_gather(coupling, 'src', axis=0, tiled=True)  39.5 us
    reduce_scatter x1, waiting for transfers between devices, on_device(): lax.psum_scatter(partial_root, 'sub', scatter_dimension=0, tiled=True)  30.1 us
    all_gather x1, waiting for transfers between devices, on_device(): lax.all_gather(root_out.astype(jnp.bfloat16), 'sub', axis=0, tiled=True)  20.1 us
    dot_general x2, matrix products, contract_rows(): lax.dot_general(left, right, (((0,), (0,)), ((), ())), preferred_element_...  10.7 us
    scatter-add x1, other arithmetic, on_device(): jnp.zeros((root_order, columns), jnp.float32).at[coupling_index].add(update)  7.04 us
  transfers between devices with their start and end apart: 5, of which 4 were waited for; matrix products, arithmetic and copies ran while one was open for 8% of the time, Pallas kernels for 0%

commit v1 on v0

--- a/solution.py
+++ b/solution.py
@@ -1,7 +1,360 @@
+import functools
 import jax
 import jax.numpy as jnp
 from jax import lax
+from jax.experimental import pallas as pl
+from jax.experimental.pallas import tpu as pltpu
 from jax.sharding import PartitionSpec as P
+
+MESH = pl.DeviceIdType.MESH
+F32 = jnp.float32
+BF16 = jnp.bfloat16
+
+
+def dot_t(left, right):
+    return lax.dot_general(left, right, (((1,), (1,)), ((), ())), preferred_element_type=F32)
+
+
+def dot_n(left, right):
+    return jnp.dot(left, right, preferred_element_type=F32)
+
+
+def kernel(
+    lines, rhs_ref, rrhs_ref, inv_ref, cpl_ref, rinv_ref, order_ref, rows_ref, child_out, root_out,
+    inv, cpl, root, hot, src_t, solved_t, upd_t, placed_t, give, take, rr_t, sol_t, sol_b, res_t,
+    recv, swap_s, send_z, send_y, send_x, send_c, ex_s, ex_r, bk_s, bk_r, lay,
+):
+    me, x = lax.axis_index("src"), lax.axis_index("sub")
+    core, y, z = me % 2, (me // 2) % 2, me // 4
+    strip = inv_ref.shape[0]
+    order = inv_ref.shape[1]
+    width = rinv_ref.shape[1]
+    part = root.shape[1]
+    half = order // 2
+    cols = rhs_ref.shape[1]
+    hcols = cols // 2
+    own_rows = rrhs_ref.shape[0]
+    blocks = root.shape[0]
+    tile = 256
+    here = pl.multiple_of(x * hcols, hcols)
+    there = pl.multiple_of((1 - x) * hcols, hcols)
+
+    def src_of(zz, yy, cc):
+        return (zz * 2 + yy) * 2 + cc
+
+    def dev(zz, yy, cc, xx):
+        return {"src": src_of(zz, yy, cc), "sub": xx}
+
+    barrier = pltpu.get_barrier_semaphore()
+
+    def hello(device):
+        pl.semaphore_signal(barrier, inc=1, device_id=device, device_id_type=MESH)
+
+    hello(dev(z, 1 - y, core, x))
+    hello(dev(z, y, 1 - core, x))
+    hello(dev(z, y, core, 1 - x))
+
+    @pl.when(z > 0)
+    def _():
+        hello(dev(z - 1, y, core, x))
+
+    @pl.when(z < lines - 1)
+    def _():
+        hello(dev(z + 1, y, core, x))
+
+    inner = jnp.logical_and(z > 0, z < lines - 1)
+    pl.when(inner)(lambda: pl.semaphore_wait(barrier, 5))
+    pl.when(jnp.logical_not(inner))(lambda: pl.semaphore_wait(barrier, 4))
+
+    kept = 2 * x
+    given = 3 - 2 * x
+    swapped = 2 * x + 1
+    kept_far = 2 - 2 * x
+    given_far = 1 + 2 * x
+
+    def strip_ref(which, s):
+        r = pl.multiple_of(s * strip, strip)
+        return (inv if which == 0 else cpl).at[pl.ds(r, strip), :]
+
+    def block_ref(b, s):
+        return root.at[b, :, pl.ds(pl.multiple_of(s * width, width), width)]
+
+    def lives(b, s):
+        return s * width < (b + 1) * part
+
+    def views(which, b, s):
+        if which == 0:
+            ref = strip_ref(0, s)
+            r = pl.multiple_of(s * strip, strip)
+            narrow = (s + 1) * strip <= half
+            return [(narrow, inv.at[pl.ds(r, strip), pl.ds(0, half)]), (jnp.logical_not(narrow), ref)]
+        if which == 1:
+            return [(None, strip_ref(1, s))]
+        return [(lives(b, s), block_ref(b, s))]
+
+    def under(cond, f):
+        if cond is None:
+            f()
+        else:
+            pl.when(cond)(f)
+
+    def rsem(which, b, s):
+        return recv.at[which if which < 2 else b + 2, s]
+
+    def push(which, b, s, sem, device, wait=False):
+        for cond, ref in views(which, b, s):
+            def f(ref=ref):
+                cp = pltpu.make_async_remote_copy(
+                    src_ref=ref, dst_ref=ref, send_sem=sem, recv_sem=rsem(which, b, s),
+                    device_id=device, device_id_type=MESH,
+                )
+                if wait:
+                    cp.wait_send()
+                else:
+                    cp.start()
+            under(cond, f)
+
+    def arrive(which, b, s):
+        for cond, ref in views(which, b, s):
+            def f(ref=ref):
+                pltpu.make_async_remote_copy(
+                    src_ref=ref, dst_ref=ref, send_sem=recv.at[0, 0], recv_sem=rsem(which, b, s),
+                    device_id=dev(z, y, 1 - core, x), device_id_type=MESH,
+                ).wait_recv()
+            under(cond, f)
+
+    def sends(cls, which, b, zz, far, wait):
+        yy = jnp.where(far, 1 - y, y) if not isinstance(far, bool) else (1 - y if far else y)
+        s = src_of(zz, yy, core)
+        if not far:
+            @pl.when(jnp.logical_and(zz <= z, z < lines - 1))
+            def _():
+                push(which, b, s, send_z.at[cls, 0, zz], dev(z + 1, y, core, x), wait)
+
+            @pl.when(jnp.logical_and(zz >= z, z > 0))
+            def _():
+                push(which, b, s, send_z.at[cls, 1, zz], dev(z - 1, y, core, x), wait)
+
+            push(which, b, s, send_y.at[cls, zz], dev(z, 1 - y, core, x), wait)
+        if which == 2:
+            push(which, b, s, send_x.at[cls - 2, int(far), zz], dev(z, y, core, 1 - x), wait)
+        push(which, b, s, send_c.at[cls, int(far), zz], dev(z, y, 1 - core, x), wait)
+
+    def own(cls, which, b):
+        sends(cls, which, b, z, False, False)
+
+    def relay(cls, which, b, far):
+        def step(k, _):
+            zz = z + ((k + 1) // 2) * (1 - 2 * (k % 2))
+
+            @pl.when(jnp.logical_and(zz >= 0, zz < lines))
+            def _():
+                arrive(which, b, src_of(zz, 1 - y if far else y, core))
+                sends(cls, which, b, zz, far, False)
+            return 0
+        lax.fori_loop(0 if far else 1, 2 * lines - 1, step, 0)
+
+    def over_core(which, b):
+        def step(k, _):
+            arrive(which, b, src_of(k // 2, k % 2, 1 - core))
+            return 0
+        lax.fori_loop(0, 2 * lines, step, 0)
+
+    def far_plane(cls, b):
+        def step(k, _):
+            s = src_of(k // 2, k % 2, core)
+            arrive(2, b, s)
+            push(2, b, s, send_c.at[cls, k % 2, k // 2], dev(z, y, 1 - core, x))
+            return 0
+        lax.fori_loop(0, 2 * lines, step, 0)
+
+    def swap():
+        return pltpu.make_async_remote_copy(
+            src_ref=rinv_ref.at[pl.ds(part, part), :], dst_ref=block_ref(swapped, me),
+            send_sem=swap_s, recv_sem=recv.at[2 + swapped, me],
+            device_id=dev(z, y, core, 1 - x), device_id_type=MESH,
+        )
+
+    placing = [
+        pltpu.make_async_copy(inv_ref, strip_ref(0, me), lay.at[0]),
+        pltpu.make_async_copy(cpl_ref, strip_ref(1, me), lay.at[1]),
+        pltpu.make_async_copy(rinv_ref.at[pl.ds(0, part), :], block_ref(kept, me), lay.at[2]),
+    ]
+    for copy in placing:
+        copy.start()
+    pl.when(lives(swapped, me))(lambda: swap().start())
+
+    for copy in placing:
+        copy.wait()
+    own(0, 0, None)
+    own(1, 1, None)
+
+    index = rows_ref[...]
+
+    @pl.loop(0, hot.shape[0] // tile)
+    def _(i):
+        r = pl.multiple_of(i * tile, tile)
+        at = lax.broadcasted_iota(jnp.int32, (tile, index.shape[1]), 0) + r
+        hot[pl.ds(r, tile), :] = jnp.where(at == index, 1.0, 0.0).astype(BF16)
+
+    alive = lax.broadcasted_iota(jnp.int32, (1, order), 1) < order_ref[0]
+    src_t[...] = jnp.where(alive, rhs_ref[...].T, 0.0).astype(BF16)
+    own(2, 2, kept)
+    relay(0, 0, None, False)
+    pl.when(lives(given, me))(lambda: pltpu.make_async_remote_copy(
+        src_ref=block_ref(given, me), dst_ref=block_ref(given, me), send_sem=swap_s,
+        recv_sem=recv.at[2 + given, me], device_id=dev(z, y, core, 1 - x), device_id_type=MESH,
+    ).wait_recv())
+    relay(0, 0, None, True)
+    relay(1, 1, None, False)
+    own(3, 2, given)
+    over_core(0, None)
+    low = pl.ds(0, half)
+    high = pl.ds(half, half)
+    solved_t[:, low] = jnp.where(alive[:, :half], dot_t(src_t[:, low], inv[low, low]), 0.0)
+    solved_t[:, high] = jnp.where(alive[:, half:], dot_t(src_t[...], inv[high, :]), 0.0)
+    relay(1, 1, None, True)
+    relay(2, 2, kept, False)
+    over_core(1, None)
+    upd_t[...] = dot_t(solved_t[...].astype(BF16), cpl[...]).astype(BF16)
+
+    @pl.loop(0, placed_t.shape[1] // tile)
+    def _(i):
+        r = pl.multiple_of(i * tile, tile)
+        placed_t[:, pl.ds(r, tile)] = -dot_t(upd_t[...], hot[pl.ds(r, tile), :])
+
+    mine = pl.ds(pl.multiple_of(x * own_rows, own_rows), own_rows)
+    placed_t[:, mine] += rrhs_ref[...].T
+    give[...] = placed_t[pl.ds(there, hcols), :].astype(BF16)
+    relay(2, 2, kept, True)
+
+    def exchange():
+        return pltpu.make_async_remote_copy(
+            src_ref=give, dst_ref=take, send_sem=ex_s, recv_sem=ex_r,
+            device_id=dev(z, y, core, 1 - x), device_id_type=MESH,
+        )
+
+    exchange().start()
+    relay(3, 2, given, False)
+    relay(3, 2, given, True)
+    over_core(2, kept)
+    over_core(2, given)
+    exchange().wait()
+    take[...] = (placed_t[pl.ds(here, hcols), :] + take[...].astype(F32)).astype(BF16)
+    far_plane(4, kept_far)
+    far_plane(5, given_far)
+    over_core(2, kept_far)
+    over_core(2, given_far)
+    for b in range(blocks):
+        upto = pl.ds(0, (b + 1) * part)
+        rr_t[:, pl.ds(b * part, part)] = dot_t(take[:, upto], root[b, :, upto]).astype(BF16)
+
+    def back(a):
+        piece = sol_b.at[pl.ds(here, hcols), pl.ds(a * part, part)]
+        return pltpu.make_async_remote_copy(
+            src_ref=piece, dst_ref=piece, send_sem=bk_s.at[a], recv_sem=bk_r.at[a],
+            device_id=dev(z, y, core, 1 - x), device_id_type=MESH,
+        )
+
+    for a in reversed(range(blocks)):
+        at = pl.ds(a * part, part)
+        total = dot_n(rr_t[:, at], root[a, :, at])
+        for b in range(a + 1, blocks):
+            total += dot_n(rr_t[:, pl.ds(b * part, part)], root[b, :, at])
+        sol_t[:, at] = total
+        sol_b[pl.ds(here, hcols), at] = total.astype(BF16)
+        if a + 1 < blocks:
+            back(a + 1).start()
+
+    def finish(first):
+        rows = pl.ds(first, hcols)
+        picked = dot_n(sol_b[rows, :], hot[...]).astype(BF16)
+        pulled = dot_n(picked, cpl[...])
+        res_t[rows, :] = jnp.where(alive, solved_t[rows, :] - pulled, 0.0).astype(BF16)
+        first_half = dot_n(res_t[rows, :], inv[:, low])
+        second_half = dot_n(res_t[rows, high], inv[high, high])
+        solved_t[rows, low] = jnp.where(alive[:, :half], first_half, 0.0)
+        solved_t[rows, high] = jnp.where(alive[:, half:], second_half, 0.0)
+
+    back(0).start()
+    finish(here)
+    for a in range(blocks):
+        back(a).wait_recv()
+    finish(there)
+    child_out[...] = solved_t[...].T
+    src_t[...] = sol_b[:, mine]
+    solved_t[...] = src_t[...].astype(F32)
+    solved_t[pl.ds(here, hcols), :] = sol_t[:, mine]
+    root_out[...] = solved_t[...].T
+
+    pl.when(lives(swapped, me))(lambda: swap().wait_send())
+    for a in range(blocks):
+        back(a).wait_send()
+    for cls, which, b in ((0, 0, None), (1, 1, None), (2, 2, kept), (3, 2, given)):
+        for far in (False, True):
+            def step(zz, _, cls=cls, which=which, b=b, far=far):
+                sends(cls, which, b, zz, far, True)
+                return 0
+            lax.fori_loop(0, lines, step, 0)
+    for cls, b in ((4, kept_far), (5, given_far)):
+        def step(k, _, cls=cls, b=b):
+            push(2, b, src_of(k // 2, k % 2, core), send_c.at[cls, k % 2, k // 2],
+                 dev(z, y, 1 - core, x), True)
+            return 0
+        lax.fori_loop(0, 2 * lines, step, 0)
+
+
+def fused(child_rhs, root_rhs, child_inverse, coupling_block, root_inverse, child_orders, coupling_rows):
+    n = lax.axis_size("src")
+    lines = n // 4
+    order = child_inverse.shape[2]
+    cols = child_rhs.shape[2]
+    own_rows = root_rhs.shape[0]
+    root_order = own_rows * lax.axis_size("sub")
+    couples = coupling_block.shape[1] * n
+    vmem = pl.BlockSpec(memory_space=pltpu.VMEM)
+    smem = pl.BlockSpec(memory_space=pltpu.SMEM)
+    dma = pltpu.SemaphoreType.DMA
+    child_out, root_out = pl.pallas_call(
+        functools.partial(kernel, lines),
+        out_shape=(
+            jax.ShapeDtypeStruct((order, cols), F32),
+            jax.ShapeDtypeStruct((own_rows, cols), F32),
+        ),
+        in_specs=[vmem] * 5 + [smem, vmem],
+        out_specs=(vmem, vmem),
+        scratch_shapes=[
+            pltpu.VMEM((order, order), BF16),
+            pltpu.VMEM((couples, order), BF16),
+            pltpu.VMEM((4, root_order // 4, root_order), BF16),
+            pltpu.VMEM((root_order, couples), BF16),
+            pltpu.VMEM((cols, order), BF16),
+            pltpu.VMEM((cols, order), F32),
+            pltpu.VMEM((cols, couples), BF16),
+            pltpu.VMEM((cols, root_order), F32),
+            pltpu.VMEM((cols // 2, root_order), BF16),
+            pltpu.VMEM((cols // 2, root_order), BF16),
+            pltpu.VMEM((cols // 2, root_order), BF16),
+            pltpu.VMEM((cols // 2, root_order), F32),
+            pltpu.VMEM((cols, root_order), BF16),
+            pltpu.VMEM((cols, order), BF16),
+            dma((6, n)),
+            dma,
+            dma((4, 2, lines)),
+            dma((4, lines)),
+            dma((2, 2, lines)),
+            dma((6, 2, lines)),
+            dma,
+            dma,
+            dma((4,)),
+            dma((4,)),
+            dma((3,)),
+        ],
+        compiler_params=pltpu.CompilerParams(
+            collective_id=0, has_side_effects=True, vmem_limit_bytes=60 * 1024 * 1024
+        ),
+    )(child_rhs[0], root_rhs, child_inverse[0], coupling_block[0], root_inverse, child_orders, coupling_rows)
+    return child_out[None], root_out
 
 
 def contract_rows(left, right):
@@ -58,9 +411,18 @@
     return (child_out, root_out)
 
 
+def route(child_rhs, root_rhs, child_inverse, *rest):
+    n, subs = lax.axis_size("src"), lax.axis_size("sub")
+    order = child_inverse.shape[2]
+    fits = subs == 2 and n % 4 == 0 and n >= 8 and root_rhs.shape[0] == order == rest[0].shape[1] * n
+    fits = fits and rest[1].shape[1] % 128 == 0 and child_rhs.shape[2] % 256 == 0
+    form = fused if fits else on_device
+    return form(child_rhs, root_rhs, child_inverse, *rest)
+
+
 def solution(mesh):
     return jax.shard_map(
-        on_device,
+        route,
         mesh=mesh,
         in_specs=(
             P("sub", None, "src"),

time: 242 us -> 101 us (0.42)
  waiting for transfers between devices: 135 us -> 0 us
  Pallas kernels: 0 us -> 96.5 us
  blocking collectives: 54.1 us -> 0 us
  matrix products: 16 us -> 0 us
  between operations: 14.5 us -> 1.29 us
  other arithmetic: 12.6 us -> 0 us
  local copies, waits for them, and re-layouts: 9.44 us -> 3.32 us
    all_gather x4 -> x0, waiting for transfers between devices: 103 us -> none  [the longest x1 43.6 us: on_device(): lax.all_gather(inverse, 'src', axis=0, tiled=True)]
    pallas_call x0 -> x1, Pallas kernels: none -> 96.5 us  [fused(): pl.pallas_call(functools.partial(kernel, lines), out_shape=(jax.ShapeDtyp...]
    psum x1 -> x0, blocking collectives: 54.1 us -> none  [on_device(): root_source = lax.psum(summand, 'sub').astype(jnp.bfloat16)]
    reduce_scatter x1 -> x0, waiting for transfers between devices: 30.1 us -> none  [on_device(): lax.psum_scatter(partial_root, 'sub', scatter_dimension=0, tiled=True)]
    dot_general x4 -> x0, matrix products: 16 us -> none  [the longest x2 10.7 us: contract_rows(): lax.dot_general(left, right, (((0,), (0,)), ((), ())), preferred_element_...]
    scatter-add x1 -> x0, other arithmetic: 7.04 us -> none  [on_device(): jnp.zeros((root_order, columns), jnp.float32).at[coupling_index].add(update)]
    gather x1 -> x0, local copies, waits for them, and re-layouts: 3.94 us -> none  [on_device(): picked = rounded_all[coupling_index]]
  transfers between devices with their start and end apart: 5 -> 0, of which waited for: 4 -> 0; matrix products, arithmetic and copies ran while one was open for 8% -> 0% of each run, Pallas kernels for 0% -> 0%
where the time goes in v1:
time: 101 us
  Pallas kernels  96.5 us (96%)
  local copies, waits for them, and re-layouts  3.32 us (3%)
  between operations  1.29 us (1%)
    pallas_call x1, Pallas kernels, fused(): pl.pallas_call(functools.partial(kernel, lines), out_shape=(jax.ShapeDtyp...  96.5 us
    unnamed x4, local copies, waits for them, and re-layouts  3.32 us

profile of v1, /device:TPU:0, one launch (start us, length us, event | category | flops | bytes accessed | tf_op | source)
XLA Modules:
  0.0 101.1 jit_solution(7184992594995879617)
XLA Ops:
  1.3 96.5 %shard_map.86 = (f32[1024,256]{1,0:T(8,128)}, f32[1024,256]{1,0:T(8,128)}) custom-call(f32[1024,256]{1,0:T(8,128)} %bitcast.4, f32[1024,256]{1,0:T(8,128)} %rrhs_ref.1, bf16[64,1024]{1,0:T(8,128)(2,1)} %bitcast.6, bf16[64,1024]{1,0:T(8,128)(2,1)} %bitcast.7, bf16[1024,128]{1,0:T(8,128)(2,1)} %rinv_ref.1, s32[1]{0:T(128)S(6)} %copy.11.order_ref, ...), custom_call_target="tpu_custom_call" | custom-call | tf_op jit(solution)/shard_map/pallas_call | solution.py:318
  97.8 0.0 copy-start
  97.8 2.4 %copy.12 = f32[1,1024,256]{2,1,0:T(8,128)} copy(f32[1,1024,256]{2,1,0:T(8,128)} %bitcast.5) | data formatting | bytes 2097152
  100.2 0.0 copy-done
  100.2 1.0 copy.13
Async XLA Ops:
  97.8 2.4 %copy-start = (f32[1024,256]{1,0:T(8,128)S(1)}, f32[1024,256]{1,0:T(8,128)}, u32[]{:S(2)}) copy-start(f32[1024,256]{1,0:T(8,128)} %get-tuple-element.9) | copy-start | bytes 3145732
